TPU v7x, 32 devices: a whole 2x2x4 slice. The times are simulated.
32 devices in a mesh: group: 2 (over y), expert: 4 (over z), tensor: 2 (over core), section: 2 (over x).
Axes of the slice: x: 2, y: 2, z: 4, core: 2. Of those that a mesh axis runs over, the one named last changes fastest.
Arguments:
- tokens: bfloat16 [32, 2048], P(('group', 'expert')), parts along dimension 0, may hold values from -10 to 10
- lengths: int32 [32], P(('group', 'expert')), parts along dimension 0, may hold values from 1 to 256, as said below
- routes: int32 [2, 32, 2], P('section', ('group', 'expert')), parts along dimension 1, may hold values from 0 to 3, all different within a row
- attn_gain: float32 [2, 2048], P('section'), may hold values from 0.4 to 1.6
- w_qkv: bfloat16 [2, 2, 2048, 1536], P('section', 'tensor', None, 'expert'), may hold values from -0.5 to 0.5
- w_out: bfloat16 [2, 2048, 2048], P('section', 'tensor', 'expert'), may hold values from -0.125 to 0.125
- moe_gain: float32 [2, 2048], P('section'), may hold values from 0.4 to 1.6
- router: bfloat16 [2, 2048, 4], P('section'), may hold values from -0.125 to 0.125
- w_up: bfloat16 [2, 2048, 28672], P('section', None, ('expert', 'tensor')), may hold values from -0.125 to 0.125
- w_down: bfloat16 [2, 28672, 2048], P('section', ('expert', 'tensor')), may hold values from -0.0625 to 0.0625
- k_codes: int32 [2, 32, 16, 512], P('section', ('group', 'expert'), None, 'tensor'), parts along dimension 1, may hold values from -2147483648 to 2147483646
- k_scale: bfloat16 [2, 32, 8, 512], P('section', ('group', 'expert'), None, 'tensor'), parts along dimension 1, may hold values from 0.25 to 1
- k_zero: bfloat16 [2, 32, 8, 512], P('section', ('group', 'expert'), None, 'tensor'), parts along dimension 1, may hold values from -4 to 4
- v_codes: int32 [2, 32, 16, 512], P('section', ('group', 'expert'), None, 'tensor'), parts along dimension 1, may hold values from -2147483648 to 2147483646
- v_scale: bfloat16 [2, 32, 16, 256], P('section', ('group', 'expert'), 'tensor'), parts along dimension 1, may hold values from 0.25 to 1
- v_zero: bfloat16 [2, 32, 16, 256], P('section', ('group', 'expert'), 'tensor'), parts along dimension 1, may hold values from -4 to 4
Outputs:
- layer_outputs: bfloat16 [2, 32, 2048], P('section', ('group', 'expert')), parts along dimension 1
There are 2 independent parts, one for each index of `group`. A program takes and returns all parts, laid end to end along the dimension named above; an argument that names none is the same for every part. Nothing has to cross between parts.
Inputs may be any that keep to these rules, and one draw needn't show every extreme that they name: Each sequence has cached positions 0 to lengths - 1 and its new token stands at position lengths; some sequence has all 256. `routes`: the two experts of a token differ. `k_codes`: word w holds the codes of positions 16 * w to 16 * w + 15, position 16 * w + i in bits 2 * i and 2 * i + 1. `v_codes`: packed as the key codes.
All inputs are finite; a program needn't handle non-finite values.
Results may differ from a plain program's by a relative error of at most 0.015.
Values may be sent and summed in bfloat16 or wider, within the bound.
No kernel may reach another device: no remote copies, remote signals or barrier semaphores. Data moves between devices by JAX's collectives and lax.ppermute only.
A program may use at most 64 MiB of HBM per device.

v0:
```python
import math
import jax
import jax.numpy as jnp
from jax import lax
from jax.sharding import PartitionSpec as P

HEAD_DIM = 128
EXPERTS = 4
MB = 2
rope_base = 1000000.0
norm_eps = 1e-05


def passed_along(array, axis, by):
    count = lax.axis_size(axis)
    pairs = [(i, i + by) for i in range(count) if 0 <= i + by < count]
    return lax.ppermute(array, axis, pairs)


def rms_scale(values, gain_row):
    widened = values.astype(jnp.float32)
    return (
        widened
        * lax.rsqrt(jnp.mean(widened * widened, axis=-1, keepdims=True) + norm_eps)
        * gain_row
    )


def rotate(vector, angles):
    half_width = vector.shape[-1] // 2
    front_half = vector[..., :half_width]
    back_half = vector[..., half_width:]
    cosine_val = jnp.cos(angles)
    sine_val = jnp.sin(angles)
    return jnp.concatenate(
        [
            front_half * cosine_val - back_half * sine_val,
            back_half * cosine_val + front_half * sine_val,
        ],
        axis=-1,
    )


def unpack(packed):
    shifts = 2 * jnp.arange(16, dtype=jnp.int32)
    code_vals = jnp.bitwise_and(
        jnp.right_shift(packed[:, :, None, :], shifts[None, None, :, None]), 3
    )
    return code_vals.reshape(packed.shape[0], packed.shape[1] * 16, packed.shape[2])


def dequant_keys(packed, scales, zero_table):
    code_vals = unpack(packed).astype(jnp.float32)
    seq_count, positions, channels = code_vals.shape
    grouped = code_vals.reshape(seq_count, scales.shape[1], positions // scales.shape[1], channels)
    dequant = (
        grouped * scales.astype(jnp.float32)[:, :, None, :]
        + zero_table.astype(jnp.float32)[:, :, None, :]
    )
    return dequant.reshape(seq_count, positions, channels).astype(jnp.bfloat16)


def dequant_values(packed, scales, zero_table):
    code_vals = unpack(packed).astype(jnp.float32)
    seq_count, positions, channels = code_vals.shape
    groups = scales.shape[1]
    grouped = code_vals.reshape(seq_count, positions, groups, channels // groups)
    scale_turned = jnp.transpose(scales.astype(jnp.float32), (0, 2, 1))[:, :, :, None]
    zero_turned = jnp.transpose(zero_table.astype(jnp.float32), (0, 2, 1))[:, :, :, None]
    dequant = grouped * scale_turned + zero_turned
    return dequant.reshape(seq_count, positions, channels).astype(jnp.bfloat16)


def attend(queries, own_key, own_value, key_cache, value_cache, seq_lengths):
    scale_root = math.sqrt(queries.shape[-1])
    scores = (
        jnp.einsum("skrd,spkd->skrp", queries, key_cache, preferred_element_type=jnp.float32)
        / scale_root
    )
    own_score = (
        jnp.einsum("skrd,skd->skr", queries, own_key, preferred_element_type=jnp.float32)
        / scale_root
    )
    visible = (jnp.arange(key_cache.shape[1], dtype=jnp.int32)[None, :] < seq_lengths[:, None])[
        :, None, None, :
    ]
    highest = jnp.maximum(jnp.max(jnp.where(visible, scores, -1e30), axis=-1), own_score)
    exponents = jnp.where(visible, jnp.exp(scores - highest[..., None]), 0.0)
    own_exp = jnp.exp(own_score - highest)
    denominator = jnp.sum(exponents, axis=-1) + own_exp
    probabilities = (exponents / denominator[..., None]).astype(jnp.bfloat16)
    own_prob = (own_exp / denominator).astype(jnp.bfloat16)
    mixture = jnp.einsum(
        "skrp,spkd->skrd", probabilities, value_cache, preferred_element_type=jnp.float32
    )
    mixture = (
        mixture
        + own_prob.astype(jnp.float32)[..., None] * own_value.astype(jnp.float32)[:, :, None, :]
    )
    return mixture.astype(jnp.bfloat16).reshape(queries.shape[0], -1)


def per_device(
    tokens,
    lengths,
    routes,
    attn_gain,
    w_qkv,
    w_out,
    moe_gain,
    router,
    w_up,
    w_down,
    k_codes,
    k_scale,
    k_zero,
    v_codes,
    v_scale,
    v_zero,
):
    section_index = lax.axis_index("section")
    section_count = lax.axis_size("section")
    expert_devs = lax.axis_size("expert")
    group_size = expert_devs // EXPERTS
    seq_dev, model_width = tokens.shape
    per_block = seq_dev // MB
    kv_local = k_codes.shape[3] // HEAD_DIM
    q_local = w_out.shape[1] // HEAD_DIM
    group_ratio = q_local // kv_local
    qkv_weight = w_qkv[0, 0]
    out_weight = w_out[0]
    up_weight = w_up[0]
    down_weight = w_down[0]
    router_weight = router[0]
    attn_row = attn_gain[0]
    moe_row = moe_gain[0]
    frequency = jnp.power(rope_base, -2.0 * jnp.arange(HEAD_DIM // 2, dtype=jnp.float32) / HEAD_DIM)
    owner_expert = jnp.arange(expert_devs, dtype=jnp.int32) // group_size
    token_blocks = tokens.reshape(MB, per_block, model_width)
    incoming = jnp.zeros((per_block, model_width), jnp.bfloat16)
    results = jnp.zeros((MB, per_block, model_width), jnp.bfloat16)
    slot_ids = jnp.arange(MB, dtype=jnp.int32)
    total_ticks = MB + section_count - 1
    for tick_index in range(total_ticks):
        block_number = tick_index - section_index
        current_block = jnp.clip(block_number, 0, MB - 1)
        if tick_index < MB:
            fresh_rows = token_blocks[tick_index]
        else:
            fresh_rows = jnp.zeros_like(incoming)
        inputs = jnp.where(section_index == 0, fresh_rows, incoming)
        first_seq = current_block * per_block

        def take_rows(array_in):
            return lax.dynamic_slice_in_dim(array_in, first_seq, per_block, 0)

        seq_lengths = take_rows(lengths)
        route = take_rows(routes[0])
        normed = rms_scale(inputs, attn_row).astype(jnp.bfloat16)
        qkv_cols = jnp.dot(
            lax.all_gather(normed, "expert", axis=0, tiled=True),
            qkv_weight,
            preferred_element_type=jnp.float32,
        ).astype(jnp.bfloat16)
        qkv_rows = lax.all_to_all(qkv_cols, "expert", split_axis=0, concat_axis=1, tiled=True)
        queries = qkv_rows[:, : q_local * HEAD_DIM].reshape(
            per_block, kv_local, group_ratio, HEAD_DIM
        )
        new_keys = qkv_rows[:, q_local * HEAD_DIM : (q_local + kv_local) * HEAD_DIM].reshape(
            per_block, kv_local, HEAD_DIM
        )
        new_values = qkv_rows[:, (q_local + kv_local) * HEAD_DIM :].reshape(
            per_block, kv_local, HEAD_DIM
        )
        angles = seq_lengths.astype(jnp.float32)[:, None] * frequency[None, :]
        query_rot = rotate(queries.astype(jnp.float32), angles[:, None, None, :]).astype(
            jnp.bfloat16
        )
        key_rot = rotate(new_keys.astype(jnp.float32), angles[:, None, :]).astype(jnp.bfloat16)
        key_cache = dequant_keys(take_rows(k_codes[0]), take_rows(k_scale[0]), take_rows(k_zero[0]))
        value_cache = dequant_values(
            take_rows(v_codes[0]), take_rows(v_scale[0]), take_rows(v_zero[0])
        )
        positions = key_cache.shape[1]
        key_cache = key_cache.reshape(per_block, positions, kv_local, HEAD_DIM)
        value_cache = value_cache.reshape(per_block, positions, kv_local, HEAD_DIM)
        attended = attend(query_rot, key_rot, new_values, key_cache, value_cache, seq_lengths)
        out_cols = jnp.dot(
            lax.all_gather(attended, "expert", axis=0, tiled=True),
            out_weight,
            preferred_element_type=jnp.float32,
        )
        out_part = lax.all_to_all(out_cols, "expert", split_axis=0, concat_axis=1, tiled=True)
        out_full = lax.psum(out_part, "tensor")
        hidden = (inputs.astype(jnp.float32) + out_full).astype(jnp.bfloat16)
        moe_in = rms_scale(hidden, moe_row).astype(jnp.bfloat16)
        logits = jnp.dot(moe_in, router_weight, preferred_element_type=jnp.float32)
        chosen = route[:, :, None] == jnp.arange(EXPERTS, dtype=jnp.int32)[None, None, :]
        picked = jnp.sum(jnp.where(chosen, logits[:, None, :], 0.0), axis=-1)
        gate_first = 1.0 / (1.0 + jnp.exp(picked[:, 1] - picked[:, 0]))
        gate_second = 1.0 / (1.0 + jnp.exp(picked[:, 0] - picked[:, 1]))
        hit_first = route[None, :, 0] == owner_expert[:, None]
        hit_second = route[None, :, 1] == owner_expert[:, None]
        sending = jnp.where(
            (hit_first | hit_second)[:, :, None], moe_in[None, :, :], jnp.zeros((), jnp.bfloat16)
        )
        up_proj = jnp.einsum(
            "jcd,df->jcf",
            lax.all_to_all(sending, "expert", split_axis=0, concat_axis=0, tiled=True),
            up_weight,
            preferred_element_type=jnp.float32,
        )
        active = jax.nn.silu(up_proj).astype(jnp.bfloat16)
        partial_value = jnp.einsum(
            "jcf,fd->jcd", active, down_weight, preferred_element_type=jnp.float32
        ).astype(jnp.bfloat16)
        weight = jnp.where(hit_first, gate_first[None, :], 0.0) + jnp.where(
            hit_second, gate_second[None, :], 0.0
        )
        returned = lax.all_to_all(partial_value, "expert", split_axis=0, concat_axis=0, tiled=True)
        moe_part = jnp.sum(weight[:, :, None] * returned.astype(jnp.float32), axis=0)
        moe_out = lax.psum(moe_part, "tensor")
        output = (hidden.astype(jnp.float32) + moe_out).astype(jnp.bfloat16)
        keep_mask = (block_number >= 0) & (block_number < MB) & (slot_ids == current_block)
        results = jnp.where(keep_mask[:, None, None], output[None, :, :], results)
        if tick_index + 1 < total_ticks:
            incoming = passed_along(output, "section", 1)
    return results.reshape(1, seq_dev, model_width)


def solution(mesh):
    return jax.shard_map(
        per_device,
        mesh=mesh,
        in_specs=(
            P(("group", "expert"), None),
            P(("group", "expert")),
            P("section", ("group", "expert"), None),
            P("section", None),
            P("section", "tensor", None, "expert"),
            P("section", "tensor", "expert"),
            P("section", None),
            P("section", None, None),
            P("section", None, ("expert", "tensor")),
            P("section", ("expert", "tensor"), None),
            P("section", ("group", "expert"), None, "tensor"),
            P("section", ("group", "expert"), None, "tensor"),
            P("section", ("group", "expert"), None, "tensor"),
            P("section", ("group", "expert"), None, "tensor"),
            P("section", ("group", "expert"), "tensor", None),
            P("section", ("group", "expert"), "tensor", None),
        ),
        out_specs=P("section", ("group", "expert"), None),
        check_vma=False,
    )
```

profile of v0, /device:TPU:0, one launch (start us, length us, event | category | flops | bytes accessed | tf_op | source)
XLA Modules:
  0.0 329.7 jit_solution(4514468630163313030)
XLA Ops:
  1.9 14.9 %all-gather = bf16[4,2,2048]{2,1,0:T(2,128)(2,1)S(1)} all-gather(bf16[1,2,2048]{2,1,0:T(2,128)(2,1)S(1)} %fusion.149), channel_id=1, replica_groups=mesh['group'=2,'expert'=4,'tensor'=2,'section'=2] {'expert'}, dimensions={0}, use_global_device_ids=true | all-gather | bytes 40960 | tf_op jit(solution)/shard_map/all_gather | solution.py:161
  17.7 4.6 %all-to-all-start = ((bf16[4,2,384]{2,1,0:T(2,128)(2,1)}), bf16[4,2,384]{2,1,0:T(2,128)(2,1)S(1)}, u32[]{:S(2)}, u32[]{:S(2)}) async-start(bf16[4,2,384]{2,1,0:T(2,128)(2,1)} %all_to_all.96), calls=%async_computation | async-start | bytes 12288 | tf_op jit(solution)/shard_map/all_to_all | solution.py:165
  52.1 13.8 %all-gather.1 = bf16[4,2,1024]{2,1,0:T(2,128)(2,1)S(1)} all-gather(bf16[1,2,1024]{2,1,0:T(2,128)(2,1)S(1)} %reshape.1245), channel_id=1, replica_groups=mesh['group'=2,'expert'=4,'tensor'=2,'section'=2] {'expert'}, dimensions={0}, use_global_device_ids=true | all-gather | bytes 20480 | tf_op jit(solution)/shard_map/all_gather | solution.py:189
  66.8 4.5 %all-to-all-start.1 = ((f32[4,2,512]{2,1,0:T(2,128)}), f32[4,2,512]{2,1,0:T(2,128)S(1)}, u32[]{:S(2)}, u32[]{:S(2)}) async-start(f32[4,2,512]{2,1,0:T(2,128)} %fusion.43), calls=%async_computation.1 | async-start | bytes 32768 | tf_op jit(solution)/shard_map/all_to_all | solution.py:193
  73.4 3.5 %all-to-all-done.1 = f32[4,2,512]{2,1,0:T(2,128)S(1)} async-done(((f32[4,2,512]{2,1,0:T(2,128)}), f32[4,2,512]{2,1,0:T(2,128)S(1)}, u32[]{:S(2)}, u32[]{:S(2)}) %all-to-all-start.1) | async-done | bytes 16416 | tf_op jit(solution)/shard_map/all_to_all | solution.py:193
  76.9 3.3 %psum.42 = f32[2,2048]{1,0:T(2,128)S(1)} all-reduce(f32[2,2048]{1,0:T(2,128)S(1)} %bitcast.222), channel_id=1, replica_groups=mesh['group'=2,'expert'=4,'tensor'=2,'section'=2] {'tensor'}, use_global_device_ids=true, to_apply=%region_3.4 | all-reduce | flops 4096 | bytes 32768 | tf_op jit(solution)/shard_map/psum | solution.py:194
  82.2 3.3 all-to-all-start.2
  85.7 5.4 %all-to-all-done.2 = bf16[4,2,2048]{2,1,0:T(2,128)(2,1)S(1)} async-done(((bf16[4,2,2048]{2,1,0:T(2,128)(2,1)}), bf16[4,2,2048]{2,1,0:T(2,128)(2,1)S(1)}, u32[]{:S(2)}, u32[]{:S(2)}) %all-to-all-start.2) | async-done | bytes 32800 | tf_op jit(solution)/shard_map/all_to_all | solution.py:209
  91.1 11.6 %fusion.12 = bf16[4,2,2048]{2,0,1:T(4,128)(2,1)S(1)} fusion(bf16[1,3584,2048]{2,1,0:T(8,128)(2,1)} %param.25, bf16[1,2048,3584]{2,1,0:T(8,128)(2,1)} %param.24, bf16[4,2,2048]{2,1,0:T(2,128)(2,1)S(1)} %all-to-all-done.2), kind=kOutput, calls=%fused_computation.12 | convolution fusion | flops 235040768 | bytes 29425664 | tf_op jit(solution)/shard_map/jcf,fd->jcd/dot_general | solution.py:214
  106.6 5.6 %all-to-all-done.3 = bf16[4,2,2048]{2,1,0:T(2,128)(2,1)S(1)} async-done(((bf16[4,2,2048]{2,1,0:T(2,128)(2,1)}), bf16[4,2,2048]{2,1,0:T(2,128)(2,1)S(1)}, u32[]{:S(2)}, u32[]{:S(2)}) %all-to-all-start.3) | async-done | bytes 32800 | tf_op jit(solution)/shard_map/all_to_all | solution.py:220
  112.3 3.4 %psum.43 = f32[2,2048]{1,0:T(2,128)S(1)} all-reduce(f32[2,2048]{1,0:T(2,128)S(1)} %multiply_reduce_fusion.2), channel_id=1, replica_groups=mesh['group'=2,'expert'=4,'tensor'=2,'section'=2] {'tensor'}, use_global_device_ids=true, to_apply=%region_7.8 | all-reduce | flops 4096 | bytes 32768 | tf_op jit(solution)/shard_map/psum | solution.py:222
  115.7 3.4 %collective-permute-start = (bf16[2,2048]{1,0:T(2,128)(2,1)S(1)}, bf16[2,2048]{1,0:T(2,128)(2,1)S(1)}, u32[]{:S(2)}, u32[]{:S(2)}) collective-permute-start(bf16[2,2048]{1,0:T(2,128)(2,1)S(1)} %fusion.112), channel_id=1, source_target_pairs={{0,1},{2,3},{4,5},{6,7},{8,9},{10,11},{12,13},{14,15},{16,17},{18,... | collective-permute-start | bytes 24584 | tf_op jit(solution)/shard_map/ppermute | solution.py:17
  120.7 13.1 %all-gather.2 = bf16[4,2,2048]{2,1,0:T(2,128)(2,1)S(1)} all-gather(bf16[1,2,2048]{2,1,0:T(2,128)(2,1)S(1)} %fusion.148), channel_id=1, replica_groups=mesh['group'=2,'expert'=4,'tensor'=2,'section'=2] {'expert'}, dimensions={0}, use_global_device_ids=true | all-gather | bytes 40960 | tf_op jit(solution)/shard_map/all_gather | solution.py:161
  158.7 13.7 %all-gather.3 = bf16[4,2,1024]{2,1,0:T(2,128)(2,1)S(1)} all-gather(bf16[1,2,1024]{2,1,0:T(2,128)(2,1)S(1)} %reshape.1249), channel_id=1, replica_groups=mesh['group'=2,'expert'=4,'tensor'=2,'section'=2] {'expert'}, dimensions={0}, use_global_device_ids=true | all-gather | bytes 20480 | tf_op jit(solution)/shard_map/all_gather | solution.py:189
  173.3 4.5 %all-to-all-start.5 = ((f32[4,2,512]{2,1,0:T(2,128)}), f32[4,2,512]{2,1,0:T(2,128)S(1)}, u32[]{:S(2)}, u32[]{:S(2)}) async-start(f32[4,2,512]{2,1,0:T(2,128)} %fusion.41), calls=%async_computation.5 | async-start | bytes 32768 | tf_op jit(solution)/shard_map/all_to_all | solution.py:193
  177.9 5.6 %all-to-all-done.5 = f32[4,2,512]{2,1,0:T(2,128)S(1)} async-done(((f32[4,2,512]{2,1,0:T(2,128)}), f32[4,2,512]{2,1,0:T(2,128)S(1)}, u32[]{:S(2)}, u32[]{:S(2)}) %all-to-all-start.5) | async-done | bytes 16416 | tf_op jit(solution)/shard_map/all_to_all | solution.py:193
  183.5 3.3 %psum.44 = f32[2,2048]{1,0:T(2,128)S(1)} all-reduce(f32[2,2048]{1,0:T(2,128)S(1)} %bitcast.221), channel_id=1, replica_groups=mesh['group'=2,'expert'=4,'tensor'=2,'section'=2] {'tensor'}, use_global_device_ids=true, to_apply=%region_11.12 | all-reduce | flops 4096 | bytes 32768 | tf_op jit(solution)/shard_map/psum | solution.py:194
  188.8 3.4 %all-to-all-start.6 = ((bf16[4,2,2048]{2,1,0:T(2,128)(2,1)}), bf16[4,2,2048]{2,1,0:T(2,128)(2,1)S(1)}, u32[]{:S(2)}, u32[]{:S(2)}) async-start(bf16[4,2,2048]{2,1,0:T(2,128)(2,1)} %broadcast_select_fusion.1), calls=%async_computation.6 | async-start | bytes 65536 | tf_op jit(solution)/shard_map/all_to_all | solution.py:209
  192.4 5.2 %all-to-all-done.6 = bf16[4,2,2048]{2,1,0:T(2,128)(2,1)S(1)} async-done(((bf16[4,2,2048]{2,1,0:T(2,128)(2,1)}), bf16[4,2,2048]{2,1,0:T(2,128)(2,1)S(1)}, u32[]{:S(2)}, u32[]{:S(2)}) %all-to-all-start.6) | async-done | bytes 32800 | tf_op jit(solution)/shard_map/all_to_all | solution.py:209
  197.7 11.6 %fusion.15 = bf16[4,2,2048]{2,0,1:T(4,128)(2,1)S(1)} fusion(bf16[1,3584,2048]{2,1,0:T(8,128)(2,1)} %param.25, bf16[1,2048,3584]{2,1,0:T(8,128)(2,1)} %param.24, bf16[4,2,2048]{2,1,0:T(2,128)(2,1)S(1)} %all-to-all-done.6), kind=kOutput, calls=%fused_computation.13 | convolution fusion | flops 235040768 | bytes 29425664 | tf_op jit(solution)/shard_map/jcf,fd->jcd/dot_general | solution.py:214
  213.2 5.6 %all-to-all-done.7 = bf16[4,2,2048]{2,1,0:T(2,128)(2,1)S(1)} async-done(((bf16[4,2,2048]{2,1,0:T(2,128)(2,1)}), bf16[4,2,2048]{2,1,0:T(2,128)(2,1)S(1)}, u32[]{:S(2)}, u32[]{:S(2)}) %all-to-all-start.7) | async-done | bytes 32800 | tf_op jit(solution)/shard_map/all_to_all | solution.py:220
  218.9 3.4 %psum.45 = f32[2,2048]{1,0:T(2,128)S(1)} all-reduce(f32[2,2048]{1,0:T(2,128)S(1)} %multiply_reduce_fusion.1), channel_id=1, replica_groups=mesh['group'=2,'expert'=4,'tensor'=2,'section'=2] {'tensor'}, use_global_device_ids=true, to_apply=%region_15.16 | all-reduce | flops 4096 | bytes 32768 | tf_op jit(solution)/shard_map/psum | solution.py:222
  222.3 4.2 %collective-permute-start.1 = (bf16[2,2048]{1,0:T(2,128)(2,1)S(1)}, bf16[2,2048]{1,0:T(2,128)(2,1)S(1)}, u32[]{:S(2)}, u32[]{:S(2)}) collective-permute-start(bf16[2,2048]{1,0:T(2,128)(2,1)S(1)} %fusion.120), channel_id=1, source_target_pairs={{0,1},{2,3},{4,5},{6,7},{8,9},{10,11},{12,13},{14,15},{16,17},{18,... | collective-permute-start | bytes 24584 | tf_op jit(solution)/shard_map/ppermute | solution.py:17
  228.1 13.1 %all-gather.4 = bf16[4,2,2048]{2,1,0:T(2,128)(2,1)S(1)} all-gather(bf16[1,2,2048]{2,1,0:T(2,128)(2,1)S(1)} %fusion.147), channel_id=1, replica_groups=mesh['group'=2,'expert'=4,'tensor'=2,'section'=2] {'expert'}, dimensions={0}, use_global_device_ids=true | all-gather | bytes 40960 | tf_op jit(solution)/shard_map/all_gather | solution.py:161
  266.2 13.7 %all-gather.5 = bf16[4,2,1024]{2,1,0:T(2,128)(2,1)S(1)} all-gather(bf16[1,2,1024]{2,1,0:T(2,128)(2,1)S(1)} %reshape.1253), channel_id=1, replica_groups=mesh['group'=2,'expert'=4,'tensor'=2,'section'=2] {'expert'}, dimensions={0}, use_global_device_ids=true | all-gather | bytes 20480 | tf_op jit(solution)/shard_map/all_gather | solution.py:189
  280.8 4.5 %all-to-all-start.9 = ((f32[4,2,512]{2,1,0:T(2,128)}), f32[4,2,512]{2,1,0:T(2,128)S(1)}, u32[]{:S(2)}, u32[]{:S(2)}) async-start(f32[4,2,512]{2,1,0:T(2,128)} %fusion.39), calls=%async_computation.9 | async-start | bytes 32768 | tf_op jit(solution)/shard_map/all_to_all | solution.py:193
  285.9 5.0 %all-to-all-done.9 = f32[4,2,512]{2,1,0:T(2,128)S(1)} async-done(((f32[4,2,512]{2,1,0:T(2,128)}), f32[4,2,512]{2,1,0:T(2,128)S(1)}, u32[]{:S(2)}, u32[]{:S(2)}) %all-to-all-start.9) | async-done | bytes 16416 | tf_op jit(solution)/shard_map/all_to_all | solution.py:193
  290.9 3.3 %psum.46 = f32[2,2048]{1,0:T(2,128)S(1)} all-reduce(f32[2,2048]{1,0:T(2,128)S(1)} %bitcast.220), channel_id=1, replica_groups=mesh['group'=2,'expert'=4,'tensor'=2,'section'=2] {'tensor'}, use_global_device_ids=true, to_apply=%region_19.20 | all-reduce | flops 4096 | bytes 32768 | tf_op jit(solution)/shard_map/psum | solution.py:194
  299.0 5.4 %all-to-all-done.10 = bf16[4,2,2048]{2,1,0:T(2,128)(2,1)S(1)} async-done(((bf16[4,2,2048]{2,1,0:T(2,128)(2,1)}), bf16[4,2,2048]{2,1,0:T(2,128)(2,1)S(1)}, u32[]{:S(2)}, u32[]{:S(2)}) %all-to-all-start.10) | async-done | bytes 32800 | tf_op jit(solution)/shard_map/all_to_all | solution.py:209
  304.4 11.6 %fusion.18 = bf16[4,2,2048]{2,0,1:T(4,128)(2,1)S(1)} fusion(bf16[1,3584,2048]{2,1,0:T(8,128)(2,1)} %param.25, bf16[1,2048,3584]{2,1,0:T(8,128)(2,1)} %param.24, bf16[4,2,2048]{2,1,0:T(2,128)(2,1)S(1)} %all-to-all-done.10), kind=kOutput, calls=%fused_computation.14 | convolution fusion | flops 235040768 | bytes 29425664 | tf_op jit(solution)/shard_map/jcf,fd->jcd/dot_general | solution.py:214
  319.9 5.6 %all-to-all-done.11 = bf16[4,2,2048]{2,1,0:T(2,128)(2,1)S(1)} async-done(((bf16[4,2,2048]{2,1,0:T(2,128)(2,1)}), bf16[4,2,2048]{2,1,0:T(2,128)(2,1)S(1)}, u32[]{:S(2)}, u32[]{:S(2)}) %all-to-all-start.11) | async-done | bytes 32800 | tf_op jit(solution)/shard_map/all_to_all | solution.py:220
  325.6 3.4 %psum.47 = f32[2,2048]{1,0:T(2,128)S(1)} all-reduce(f32[2,2048]{1,0:T(2,128)S(1)} %multiply_reduce_fusion), channel_id=1, replica_groups=mesh['group'=2,'expert'=4,'tensor'=2,'section'=2] {'tensor'}, use_global_device_ids=true, to_apply=%region_23.24 | all-reduce | flops 4096 | bytes 32768 | tf_op jit(solution)/shard_map/psum | solution.py:222
  (206 shorter events, 112.5 us)
Async XLA Ops:
  0.0 16.7 %copy-start = (bf16[1,1,2048,384]{3,2,1,0:T(8,128)(2,1)S(1)}, bf16[1,1,2048,384]{3,2,1,0:T(8,128)(2,1)}, u32[]{:S(2)}) copy-start(bf16[1,1,2048,384]{3,2,1,0:T(8,128)(2,1)} %param.20) | copy-start | bytes 4718596
  0.0 80.2 %copy-start.4 = (bf16[4,2048]{1,0:T(4,128)(2,1)S(1)}, bf16[4,2048]{1,0:T(4,128)(2,1)}, u32[]{:S(2)}) copy-start(bf16[4,2048]{1,0:T(4,128)(2,1)} %param.16) | copy-start | bytes 49156
  0.0 65.9 %copy-start.1 = (bf16[1,1024,512]{2,1,0:T(8,128)(2,1)S(1)}, bf16[1,1024,512]{2,1,0:T(8,128)(2,1)}, u32[]{:S(2)}) copy-start(bf16[1,1024,512]{2,1,0:T(8,128)(2,1)} %param.21) | copy-start | bytes 3145732
  0.0 80.4 %copy-start.3 = (f32[1,2048]{1,0:T(1,128)S(1)}, f32[1,2048]{1,0:T(1,128)}, u32[]{:S(2)}) copy-start(f32[1,2048]{1,0:T(1,128)} %param.22) | copy-start | bytes 24580
  17.7 29.2 %all-to-all-start = ((bf16[4,2,384]{2,1,0:T(2,128)(2,1)}), bf16[4,2,384]{2,1,0:T(2,128)(2,1)S(1)}, u32[]{:S(2)}, u32[]{:S(2)}) async-start(bf16[4,2,384]{2,1,0:T(2,128)(2,1)} %all_to_all.96), calls=%async_computation | async-start | bytes 12288 | tf_op jit(solution)/shard_map/all_to_all | solution.py:165
  66.8 10.1 %all-to-all-start.1 = ((f32[4,2,512]{2,1,0:T(2,128)}), f32[4,2,512]{2,1,0:T(2,128)S(1)}, u32[]{:S(2)}, u32[]{:S(2)}) async-start(f32[4,2,512]{2,1,0:T(2,128)} %fusion.43), calls=%async_computation.1 | async-start | bytes 32768 | tf_op jit(solution)/shard_map/all_to_all | solution.py:193
  82.2 8.9 %all-to-all-start.2 = ((bf16[4,2,2048]{2,1,0:T(2,128)(2,1)}), bf16[4,2,2048]{2,1,0:T(2,128)(2,1)S(1)}, u32[]{:S(2)}, u32[]{:S(2)}) async-start(bf16[4,2,2048]{2,1,0:T(2,128)(2,1)} %broadcast_select_fusion.2), calls=%async_computation.2 | async-start | bytes 65536 | tf_op jit(solution)/shard_map/all_to_all | solution.py:209
  85.7 20.9 %copy-start.9 = (s32[2]{0:T(128)S(1)}, s32[2]{0:T(128)}, u32[]{:S(2)}) copy-start(s32[2]{0:T(128)} %get-tuple-element.11) | copy-start | bytes 28
  85.7 20.9 %copy-start.10 = (s32[2]{0:T(128)S(1)}, s32[2]{0:T(128)}, u32[]{:S(2)}) copy-start(s32[2]{0:T(128)} %get-tuple-element.12) | copy-start | bytes 28
  85.7 34.9 %copy-start.2 = (f32[1,2048]{1,0:T(1,128)S(1)}, f32[1,2048]{1,0:T(1,128)}, u32[]{:S(2)}) copy-start(f32[1,2048]{1,0:T(1,128)} %param.19) | copy-start | bytes 24580
  85.7 69.1 %copy-start.7 = (f32[2,64]{1,0:T(2,128)S(1)}, f32[2,64]{1,0:T(2,128)}, u32[]{:S(2)}) copy-start(f32[2,64]{1,0:T(2,128)} %get-tuple-element.82) | copy-start | bytes 1540
  85.7 69.1 %copy-start.8 = (f32[2,64]{1,0:T(2,128)S(1)}, f32[2,64]{1,0:T(2,128)}, u32[]{:S(2)}) copy-start(f32[2,64]{1,0:T(2,128)} %get-tuple-element.83) | copy-start | bytes 1540
  103.3 8.9 %all-to-all-start.3 = ((bf16[4,2,2048]{2,1,0:T(2,128)(2,1)}), bf16[4,2,2048]{2,1,0:T(2,128)(2,1)S(1)}, u32[]{:S(2)}, u32[]{:S(2)}) async-start(bf16[4,2,2048]{2,1,0:T(2,128)(2,1)} %copy.138), calls=%async_computation.3 | async-start | bytes 65536 | tf_op jit(solution)/shard_map/all_to_all | solution.py:220
  115.7 4.8 %collective-permute-start = (bf16[2,2048]{1,0:T(2,128)(2,1)S(1)}, bf16[2,2048]{1,0:T(2,128)(2,1)S(1)}, u32[]{:S(2)}, u32[]{:S(2)}) collective-permute-start(bf16[2,2048]{1,0:T(2,128)(2,1)S(1)} %fusion.112), channel_id=1, source_target_pairs={{0,1},{2,3},{4,5},{6,7},{8,9},{10,11},{12,13},{14,15},{16,17},{18,... | collective-permute-start | bytes 24584 | tf_op jit(solution)/shard_map/ppermute | solution.py:17
  134.7 20.1 %all-to-all-start.4 = ((bf16[4,2,384]{2,1,0:T(2,128)(2,1)}), bf16[4,2,384]{2,1,0:T(2,128)(2,1)S(1)}, u32[]{:S(2)}, u32[]{:S(2)}) async-start(bf16[4,2,384]{2,1,0:T(2,128)(2,1)} %all_to_all.105), calls=%async_computation.4 | async-start | bytes 12288 | tf_op jit(solution)/shard_map/all_to_all | solution.py:165
  173.3 10.1 %all-to-all-start.5 = ((f32[4,2,512]{2,1,0:T(2,128)}), f32[4,2,512]{2,1,0:T(2,128)S(1)}, u32[]{:S(2)}, u32[]{:S(2)}) async-start(f32[4,2,512]{2,1,0:T(2,128)} %fusion.41), calls=%async_computation.5 | async-start | bytes 32768 | tf_op jit(solution)/shard_map/all_to_all | solution.py:193
  188.8 8.9 %all-to-all-start.6 = ((bf16[4,2,2048]{2,1,0:T(2,128)(2,1)}), bf16[4,2,2048]{2,1,0:T(2,128)(2,1)S(1)}, u32[]{:S(2)}, u32[]{:S(2)}) async-start(bf16[4,2,2048]{2,1,0:T(2,128)(2,1)} %broadcast_select_fusion.1), calls=%async_computation.6 | async-start | bytes 65536 | tf_op jit(solution)/shard_map/all_to_all | solution.py:209
  192.4 69.8 %copy-start.5 = (f32[2,64]{1,0:T(2,128)S(1)}, f32[2,64]{1,0:T(2,128)}, u32[]{:S(2)}) copy-start(f32[2,64]{1,0:T(2,128)} %get-tuple-element.73) | copy-start | bytes 1540
  192.4 69.8 %copy-start.6 = (f32[2,64]{1,0:T(2,128)S(1)}, f32[2,64]{1,0:T(2,128)}, u32[]{:S(2)}) copy-start(f32[2,64]{1,0:T(2,128)} %get-tuple-element.74) | copy-start | bytes 1540
  209.2 85.2 %copy-start.11 = (bf16[1,2048,4]{1,2,0:T(4,128)(2,1)S(1)}, bf16[1,2048,4]{1,2,0:T(4,128)(2,1)}, u32[]{:S(2)}) copy-start(bf16[1,2048,4]{1,2,0:T(4,128)(2,1)} %param.23) | copy-start | bytes 49156
  209.9 8.9 %all-to-all-start.7 = ((bf16[4,2,2048]{2,1,0:T(2,128)(2,1)}), bf16[4,2,2048]{2,1,0:T(2,128)(2,1)S(1)}, u32[]{:S(2)}, u32[]{:S(2)}) async-start(bf16[4,2,2048]{2,1,0:T(2,128)(2,1)} %copy.149), calls=%async_computation.7 | async-start | bytes 65536 | tf_op jit(solution)/shard_map/all_to_all | solution.py:220
  222.3 5.6 %collective-permute-start.1 = (bf16[2,2048]{1,0:T(2,128)(2,1)S(1)}, bf16[2,2048]{1,0:T(2,128)(2,1)S(1)}, u32[]{:S(2)}, u32[]{:S(2)}) collective-permute-start(bf16[2,2048]{1,0:T(2,128)(2,1)S(1)} %fusion.120), channel_id=1, source_target_pairs={{0,1},{2,3},{4,5},{6,7},{8,9},{10,11},{12,13},{14,15},{16,17},{18,... | collective-permute-start | bytes 24584 | tf_op jit(solution)/shard_map/ppermute | solution.py:17
  242.1 20.1 %all-to-all-start.8 = ((bf16[4,2,384]{2,1,0:T(2,128)(2,1)}), bf16[4,2,384]{2,1,0:T(2,128)(2,1)S(1)}, u32[]{:S(2)}, u32[]{:S(2)}) async-start(bf16[4,2,384]{2,1,0:T(2,128)(2,1)} %all_to_all.114), calls=%async_computation.8 | async-start | bytes 12288 | tf_op jit(solution)/shard_map/all_to_all | solution.py:165
  280.8 10.1 %all-to-all-start.9 = ((f32[4,2,512]{2,1,0:T(2,128)}), f32[4,2,512]{2,1,0:T(2,128)S(1)}, u32[]{:S(2)}, u32[]{:S(2)}) async-start(f32[4,2,512]{2,1,0:T(2,128)} %fusion.39), calls=%async_computation.9 | async-start | bytes 32768 | tf_op jit(solution)/shard_map/all_to_all | solution.py:193
  295.5 8.9 %all-to-all-start.10 = ((bf16[4,2,2048]{2,1,0:T(2,128)(2,1)}), bf16[4,2,2048]{2,1,0:T(2,128)(2,1)S(1)}, u32[]{:S(2)}, u32[]{:S(2)}) async-start(bf16[4,2,2048]{2,1,0:T(2,128)(2,1)} %broadcast_select_fusion), calls=%async_computation.10 | async-start | bytes 65536 | tf_op jit(solution)/shard_map/all_to_all | solution.py:209
  316.6 8.9 %all-to-all-start.11 = ((bf16[4,2,2048]{2,1,0:T(2,128)(2,1)}), bf16[4,2,2048]{2,1,0:T(2,128)(2,1)S(1)}, u32[]{:S(2)}, u32[]{:S(2)}) async-start(bf16[4,2,2048]{2,1,0:T(2,128)(2,1)} %copy.160), calls=%async_computation.11 | async-start | bytes 65536 | tf_op jit(solution)/shard_map/all_to_all | solution.py:220
where the time goes:
time: 332 us; the launch traced here: 330 us
  blocking collectives  102 us (31%)
  local copies, waits for them, and re-layouts  60.5 us (18%)
  starting transfers between devices  52.1 us (16%)
  matrix products  50.3 us (15%)
  waiting for transfers between devices  49.4 us (15%)
  other arithmetic  14.4 us (4%)
    all_gather x3, blocking collectives, per_device(): lax.all_gather(attended, 'expert', axis=0, tiled=True)  41.2 us
    all_gather x3, blocking collectives, per_device(): lax.all_gather(normed, 'expert', axis=0, tiled=True)  41.1 us
    dot_general x3, matrix products, per_device(): jnp.einsum('jcf,fd->jcd', active, down_weight, preferred_element_type=jnp...  34.7 us
    shift_right_arithmetic x15, local copies, waits for them, and re-layouts, unpack(): jnp.right_shift(packed[:, :, None, :], shifts[None, None, :, None])  16.9 us
    all_to_all x3, waiting for transfers between devices, per_device(): lax.all_to_all(partial_value, 'expert', split_axis=0, concat_axis=0, tile...  16.8 us
    all_to_all x3, waiting for transfers between devices, per_device(): lax.all_to_all(sending, 'expert', split_axis=0, concat_axis=0, tiled=True)  16 us
    all_to_all x3, waiting for transfers between devices, per_device(): lax.all_to_all(out_cols, 'expert', split_axis=0, concat_axis=1, tiled=True)  14.1 us
    all_to_all x3, starting transfers between devices, per_device(): lax.all_to_all(out_cols, 'expert', split_axis=0, concat_axis=1, tiled=True)  13.6 us
  transfers between devices with their start and end apart: 14, of which 11 were waited for; matrix products, arithmetic and copies ran while one was open for 19% of the time, Pallas kernels for 0%

commit v1 on v0

--- a/solution.py
+++ b/solution.py
@@ -190,7 +190,15 @@
             out_weight,
             preferred_element_type=jnp.float32,
         )
-        out_part = lax.all_to_all(out_cols, "expert", split_axis=0, concat_axis=1, tiled=True)
+        out_part = jnp.concatenate(
+            lax.all_to_all(
+                jnp.stack(jnp.split(out_cols, lax.axis_size("expert"), 0)),
+                axis_name="expert",
+                split_axis=0,
+                concat_axis=0,
+            ),
+            1,
+        )
         out_full = lax.psum(out_part, "tensor")
         hidden = (inputs.astype(jnp.float32) + out_full).astype(jnp.bfloat16)
         moe_in = rms_scale(hidden, moe_row).astype(jnp.bfloat16)

time: 332 us -> 332 us (level)
  no operation moved by 1% of the time
where the time goes in v1:
time: 332 us; the launch traced here: 330 us
  blocking collectives  102 us (31%)
  local copies, waits for them, and re-layouts  60.6 us (18%)
  starting transfers between devices  52.1 us (16%)
  waiting for transfers between devices  49.4 us (15%)
  matrix products  48.4 us (15%)
  other arithmetic  16.3 us (5%)
    all_gather x3, blocking collectives, per_device(): lax.all_gather(attended, 'expert', axis=0, tiled=True)  41.2 us
    all_gather x3, blocking collectives, per_device(): lax.all_gather(normed, 'expert', axis=0, tiled=True)  41.1 us
    dot_general x3, matrix products, per_device(): jnp.einsum('jcf,fd->jcd', active, down_weight, preferred_element_type=jnp...  34.7 us
    shift_right_arithmetic x15, local copies, waits for them, and re-layouts, unpack(): jnp.right_shift(packed[:, :, None, :], shifts[None, None, :, None])  16.9 us
    all_to_all x3, waiting for transfers between devices, per_device(): lax.all_to_all(partial_value, 'expert', split_axis=0, concat_axis=0, tile...  16.8 us
    all_to_all x3, waiting for transfers between devices, per_device(): lax.all_to_all(sending, 'expert', split_axis=0, concat_axis=0, tiled=True)  16 us
    all_to_all x3, waiting for transfers between devices, per_device(): lax.all_to_all(jnp.stack(jnp.split(out_cols, lax.axis_size('expert'), 0))...  14.1 us
    all_to_all x3, starting transfers between devices, per_device(): lax.all_to_all(jnp.stack(jnp.split(out_cols, lax.axis_size('expert'), 0))...  13.6 us
  transfers between devices with their start and end apart: 14, of which 11 were waited for; matrix products, arithmetic and copies ran while one was open for 19% of the time, Pallas kernels for 0%

profile of v1, /device:TPU:0, one launch (start us, length us, event | category | flops | bytes accessed | tf_op | source)
XLA Modules:
  0.0 329.7 jit_solution(14290421640113036209)
XLA Ops:
  1.9 14.9 %all-gather = bf16[4,2,2048]{2,1,0:T(2,128)(2,1)S(1)} all-gather(bf16[1,2,2048]{2,1,0:T(2,128)(2,1)S(1)} %fusion.149), channel_id=1, replica_groups=mesh['group'=2,'expert'=4,'tensor'=2,'section'=2] {'expert'}, dimensions={0}, use_global_device_ids=true | all-gather | bytes 40960 | tf_op jit(solution)/shard_map/all_gather | solution.py:161
  17.7 4.6 %all-to-all-start = ((bf16[4,2,384]{2,1,0:T(2,128)(2,1)}), bf16[4,2,384]{2,1,0:T(2,128)(2,1)S(1)}, u32[]{:S(2)}, u32[]{:S(2)}) async-start(bf16[4,2,384]{2,1,0:T(2,128)(2,1)} %all_to_all.69), calls=%async_computation | async-start | bytes 12288 | tf_op jit(solution)/shard_map/all_to_all | solution.py:165
  52.1 13.8 %all-gather.1 = bf16[4,2,1024]{2,1,0:T(2,128)(2,1)S(1)} all-gather(bf16[1,2,1024]{2,1,0:T(2,128)(2,1)S(1)} %reshape.1257), channel_id=1, replica_groups=mesh['group'=2,'expert'=4,'tensor'=2,'section'=2] {'expert'}, dimensions={0}, use_global_device_ids=true | all-gather | bytes 20480 | tf_op jit(solution)/shard_map/all_gather | solution.py:189
  66.8 4.5 %all-to-all-start.1 = ((f32[4,2,512]{2,1,0:T(2,128)}), f32[4,2,512]{2,1,0:T(2,128)S(1)}, u32[]{:S(2)}, u32[]{:S(2)}) async-start(f32[4,2,512]{2,1,0:T(2,128)} %pad_maximum_fusion), calls=%async_computation.1 | async-start | bytes 32768 | tf_op jit(solution)/shard_map/all_to_all | solution.py:194
  73.5 3.5 %all-to-all-done.1 = f32[4,2,512]{2,1,0:T(2,128)S(1)} async-done(((f32[4,2,512]{2,1,0:T(2,128)}), f32[4,2,512]{2,1,0:T(2,128)S(1)}, u32[]{:S(2)}, u32[]{:S(2)}) %all-to-all-start.1) | async-done | bytes 16416 | tf_op jit(solution)/shard_map/all_to_all | solution.py:194
  76.9 3.3 %psum.42 = f32[2,2048]{1,0:T(2,128)S(1)} all-reduce(f32[2,2048]{1,0:T(2,128)S(1)} %bitcast.245), channel_id=1, replica_groups=mesh['group'=2,'expert'=4,'tensor'=2,'section'=2] {'tensor'}, use_global_device_ids=true, to_apply=%region_3.4 | all-reduce | flops 4096 | bytes 32768 | tf_op jit(solution)/shard_map/psum | solution.py:202
  82.2 3.3 all-to-all-start.2
  85.7 5.4 %all-to-all-done.2 = bf16[4,2,2048]{2,1,0:T(2,128)(2,1)S(1)} async-done(((bf16[4,2,2048]{2,1,0:T(2,128)(2,1)}), bf16[4,2,2048]{2,1,0:T(2,128)(2,1)S(1)}, u32[]{:S(2)}, u32[]{:S(2)}) %all-to-all-start.2) | async-done | bytes 32800 | tf_op jit(solution)/shard_map/all_to_all | solution.py:217
  91.1 11.6 %fusion.12 = bf16[4,2,2048]{2,0,1:T(4,128)(2,1)S(1)} fusion(bf16[1,3584,2048]{2,1,0:T(8,128)(2,1)} %param.25, bf16[1,2048,3584]{2,1,0:T(8,128)(2,1)} %param.24, bf16[4,2,2048]{2,1,0:T(2,128)(2,1)S(1)} %all-to-all-done.2), kind=kOutput, calls=%fused_computation.12 | convolution fusion | flops 235040768 | bytes 29425664 | tf_op jit(solution)/shard_map/jcf,fd->jcd/dot_general | solution.py:222
  106.6 5.6 %all-to-all-done.3 = bf16[4,2,2048]{2,1,0:T(2,128)(2,1)S(1)} async-done(((bf16[4,2,2048]{2,1,0:T(2,128)(2,1)}), bf16[4,2,2048]{2,1,0:T(2,128)(2,1)S(1)}, u32[]{:S(2)}, u32[]{:S(2)}) %all-to-all-start.3) | async-done | bytes 32800 | tf_op jit(solution)/shard_map/all_to_all | solution.py:228
  112.3 3.4 %psum.43 = f32[2,2048]{1,0:T(2,128)S(1)} all-reduce(f32[2,2048]{1,0:T(2,128)S(1)} %multiply_reduce_fusion.2), channel_id=1, replica_groups=mesh['group'=2,'expert'=4,'tensor'=2,'section'=2] {'tensor'}, use_global_device_ids=true, to_apply=%region_7.8 | all-reduce | flops 4096 | bytes 32768 | tf_op jit(solution)/shard_map/psum | solution.py:230
  115.7 3.4 %collective-permute-start = (bf16[2,2048]{1,0:T(2,128)(2,1)S(1)}, bf16[2,2048]{1,0:T(2,128)(2,1)S(1)}, u32[]{:S(2)}, u32[]{:S(2)}) collective-permute-start(bf16[2,2048]{1,0:T(2,128)(2,1)S(1)} %fusion.112), channel_id=1, source_target_pairs={{0,1},{2,3},{4,5},{6,7},{8,9},{10,11},{12,13},{14,15},{16,17},{18,... | collective-permute-start | bytes 24584 | tf_op jit(solution)/shard_map/ppermute | solution.py:17
  120.7 13.1 %all-gather.2 = bf16[4,2,2048]{2,1,0:T(2,128)(2,1)S(1)} all-gather(bf16[1,2,2048]{2,1,0:T(2,128)(2,1)S(1)} %fusion.148), channel_id=1, replica_groups=mesh['group'=2,'expert'=4,'tensor'=2,'section'=2] {'expert'}, dimensions={0}, use_global_device_ids=true | all-gather | bytes 40960 | tf_op jit(solution)/shard_map/all_gather | solution.py:161
  158.8 13.7 %all-gather.3 = bf16[4,2,1024]{2,1,0:T(2,128)(2,1)S(1)} all-gather(bf16[1,2,1024]{2,1,0:T(2,128)(2,1)S(1)} %reshape.1261), channel_id=1, replica_groups=mesh['group'=2,'expert'=4,'tensor'=2,'section'=2] {'expert'}, dimensions={0}, use_global_device_ids=true | all-gather | bytes 20480 | tf_op jit(solution)/shard_map/all_gather | solution.py:189
  173.4 4.5 %all-to-all-start.5 = ((f32[4,2,512]{2,1,0:T(2,128)}), f32[4,2,512]{2,1,0:T(2,128)S(1)}, u32[]{:S(2)}, u32[]{:S(2)}) async-start(f32[4,2,512]{2,1,0:T(2,128)} %pad_maximum_fusion.1), calls=%async_computation.5 | async-start | bytes 32768 | tf_op jit(solution)/shard_map/all_to_all | solution.py:194
  177.9 5.6 %all-to-all-done.5 = f32[4,2,512]{2,1,0:T(2,128)S(1)} async-done(((f32[4,2,512]{2,1,0:T(2,128)}), f32[4,2,512]{2,1,0:T(2,128)S(1)}, u32[]{:S(2)}, u32[]{:S(2)}) %all-to-all-start.5) | async-done | bytes 16416 | tf_op jit(solution)/shard_map/all_to_all | solution.py:194
  183.5 3.3 %psum.44 = f32[2,2048]{1,0:T(2,128)S(1)} all-reduce(f32[2,2048]{1,0:T(2,128)S(1)} %bitcast.244), channel_id=1, replica_groups=mesh['group'=2,'expert'=4,'tensor'=2,'section'=2] {'tensor'}, use_global_device_ids=true, to_apply=%region_11.12 | all-reduce | flops 4096 | bytes 32768 | tf_op jit(solution)/shard_map/psum | solution.py:202
  188.8 3.4 %all-to-all-start.6 = ((bf16[4,2,2048]{2,1,0:T(2,128)(2,1)}), bf16[4,2,2048]{2,1,0:T(2,128)(2,1)S(1)}, u32[]{:S(2)}, u32[]{:S(2)}) async-start(bf16[4,2,2048]{2,1,0:T(2,128)(2,1)} %broadcast_select_fusion.1), calls=%async_computation.6 | async-start | bytes 65536 | tf_op jit(solution)/shard_map/all_to_all | solution.py:217
  192.5 5.2 %all-to-all-done.6 = bf16[4,2,2048]{2,1,0:T(2,128)(2,1)S(1)} async-done(((bf16[4,2,2048]{2,1,0:T(2,128)(2,1)}), bf16[4,2,2048]{2,1,0:T(2,128)(2,1)S(1)}, u32[]{:S(2)}, u32[]{:S(2)}) %all-to-all-start.6) | async-done | bytes 32800 | tf_op jit(solution)/shard_map/all_to_all | solution.py:217
  197.7 11.6 %fusion.15 = bf16[4,2,2048]{2,0,1:T(4,128)(2,1)S(1)} fusion(bf16[1,3584,2048]{2,1,0:T(8,128)(2,1)} %param.25, bf16[1,2048,3584]{2,1,0:T(8,128)(2,1)} %param.24, bf16[4,2,2048]{2,1,0:T(2,128)(2,1)S(1)} %all-to-all-done.6), kind=kOutput, calls=%fused_computation.13 | convolution fusion | flops 235040768 | bytes 29425664 | tf_op jit(solution)/shard_map/jcf,fd->jcd/dot_general | solution.py:222
  213.2 5.6 %all-to-all-done.7 = bf16[4,2,2048]{2,1,0:T(2,128)(2,1)S(1)} async-done(((bf16[4,2,2048]{2,1,0:T(2,128)(2,1)}), bf16[4,2,2048]{2,1,0:T(2,128)(2,1)S(1)}, u32[]{:S(2)}, u32[]{:S(2)}) %all-to-all-start.7) | async-done | bytes 32800 | tf_op jit(solution)/shard_map/all_to_all | solution.py:228
  218.9 3.4 %psum.45 = f32[2,2048]{1,0:T(2,128)S(1)} all-reduce(f32[2,2048]{1,0:T(2,128)S(1)} %multiply_reduce_fusion.1), channel_id=1, replica_groups=mesh['group'=2,'expert'=4,'tensor'=2,'section'=2] {'tensor'}, use_global_device_ids=true, to_apply=%region_15.16 | all-reduce | flops 4096 | bytes 32768 | tf_op jit(solution)/shard_map/psum | solution.py:230
  222.3 4.2 %collective-permute-start.1 = (bf16[2,2048]{1,0:T(2,128)(2,1)S(1)}, bf16[2,2048]{1,0:T(2,128)(2,1)S(1)}, u32[]{:S(2)}, u32[]{:S(2)}) collective-permute-start(bf16[2,2048]{1,0:T(2,128)(2,1)S(1)} %fusion.120), channel_id=1, source_target_pairs={{0,1},{2,3},{4,5},{6,7},{8,9},{10,11},{12,13},{14,15},{16,17},{18,... | collective-permute-start | bytes 24584 | tf_op jit(solution)/shard_map/ppermute | solution.py:17
  228.1 13.1 %all-gather.4 = bf16[4,2,2048]{2,1,0:T(2,128)(2,1)S(1)} all-gather(bf16[1,2,2048]{2,1,0:T(2,128)(2,1)S(1)} %fusion.147), channel_id=1, replica_groups=mesh['group'=2,'expert'=4,'tensor'=2,'section'=2] {'expert'}, dimensions={0}, use_global_device_ids=true | all-gather | bytes 40960 | tf_op jit(solution)/shard_map/all_gather | solution.py:161
  266.2 13.7 %all-gather.5 = bf16[4,2,1024]{2,1,0:T(2,128)(2,1)S(1)} all-gather(bf16[1,2,1024]{2,1,0:T(2,128)(2,1)S(1)} %reshape.1265), channel_id=1, replica_groups=mesh['group'=2,'expert'=4,'tensor'=2,'section'=2] {'expert'}, dimensions={0}, use_global_device_ids=true | all-gather | bytes 20480 | tf_op jit(solution)/shard_map/all_gather | solution.py:189
  280.8 4.5 %all-to-all-start.9 = ((f32[4,2,512]{2,1,0:T(2,128)}), f32[4,2,512]{2,1,0:T(2,128)S(1)}, u32[]{:S(2)}, u32[]{:S(2)}) async-start(f32[4,2,512]{2,1,0:T(2,128)} %pad_maximum_fusion.2), calls=%async_computation.9 | async-start | bytes 32768 | tf_op jit(solution)/shard_map/all_to_all | solution.py:194
  285.9 5.0 %all-to-all-done.9 = f32[4,2,512]{2,1,0:T(2,128)S(1)} async-done(((f32[4,2,512]{2,1,0:T(2,128)}), f32[4,2,512]{2,1,0:T(2,128)S(1)}, u32[]{:S(2)}, u32[]{:S(2)}) %all-to-all-start.9) | async-done | bytes 16416 | tf_op jit(solution)/shard_map/all_to_all | solution.py:194
  291.0 3.3 %psum.46 = f32[2,2048]{1,0:T(2,128)S(1)} all-reduce(f32[2,2048]{1,0:T(2,128)S(1)} %bitcast.243), channel_id=1, replica_groups=mesh['group'=2,'expert'=4,'tensor'=2,'section'=2] {'tensor'}, use_global_device_ids=true, to_apply=%region_19.20 | all-reduce | flops 4096 | bytes 32768 | tf_op jit(solution)/shard_map/psum | solution.py:202
  299.0 5.4 %all-to-all-done.10 = bf16[4,2,2048]{2,1,0:T(2,128)(2,1)S(1)} async-done(((bf16[4,2,2048]{2,1,0:T(2,128)(2,1)}), bf16[4,2,2048]{2,1,0:T(2,128)(2,1)S(1)}, u32[]{:S(2)}, u32[]{:S(2)}) %all-to-all-start.10) | async-done | bytes 32800 | tf_op jit(solution)/shard_map/all_to_all | solution.py:217
  304.4 11.6 %fusion.18 = bf16[4,2,2048]{2,0,1:T(4,128)(2,1)S(1)} fusion(bf16[1,3584,2048]{2,1,0:T(8,128)(2,1)} %param.25, bf16[1,2048,3584]{2,1,0:T(8,128)(2,1)} %param.24, bf16[4,2,2048]{2,1,0:T(2,128)(2,1)S(1)} %all-to-all-done.10), kind=kOutput, calls=%fused_computation.14 | convolution fusion | flops 235040768 | bytes 29425664 | tf_op jit(solution)/shard_map/jcf,fd->jcd/dot_general | solution.py:222
  319.9 5.6 %all-to-all-done.11 = bf16[4,2,2048]{2,1,0:T(2,128)(2,1)S(1)} async-done(((bf16[4,2,2048]{2,1,0:T(2,128)(2,1)}), bf16[4,2,2048]{2,1,0:T(2,128)(2,1)S(1)}, u32[]{:S(2)}, u32[]{:S(2)}) %all-to-all-start.11) | async-done | bytes 32800 | tf_op jit(solution)/shard_map/all_to_all | solution.py:228
  325.6 3.4 %psum.47 = f32[2,2048]{1,0:T(2,128)S(1)} all-reduce(f32[2,2048]{1,0:T(2,128)S(1)} %multiply_reduce_fusion), channel_id=1, replica_groups=mesh['group'=2,'expert'=4,'tensor'=2,'section'=2] {'tensor'}, use_global_device_ids=true, to_apply=%region_23.24 | all-reduce | flops 4096 | bytes 32768 | tf_op jit(solution)/shard_map/psum | solution.py:230
  (215 shorter events, 112.6 us)
Async XLA Ops:
  0.0 16.7 %copy-start = (bf16[1,1,2048,384]{3,2,1,0:T(8,128)(2,1)S(1)}, bf16[1,1,2048,384]{3,2,1,0:T(8,128)(2,1)}, u32[]{:S(2)}) copy-start(bf16[1,1,2048,384]{3,2,1,0:T(8,128)(2,1)} %param.20) | copy-start | bytes 4718596
  0.0 80.3 %copy-start.4 = (bf16[4,2048]{1,0:T(4,128)(2,1)S(1)}, bf16[4,2048]{1,0:T(4,128)(2,1)}, u32[]{:S(2)}) copy-start(bf16[4,2048]{1,0:T(4,128)(2,1)} %param.16) | copy-start | bytes 49156
  0.0 65.9 %copy-start.1 = (bf16[1,1024,512]{2,1,0:T(8,128)(2,1)S(1)}, bf16[1,1024,512]{2,1,0:T(8,128)(2,1)}, u32[]{:S(2)}) copy-start(bf16[1,1024,512]{2,1,0:T(8,128)(2,1)} %param.21) | copy-start | bytes 3145732
  0.0 80.4 %copy-start.3 = (f32[1,2048]{1,0:T(1,128)S(1)}, f32[1,2048]{1,0:T(1,128)}, u32[]{:S(2)}) copy-start(f32[1,2048]{1,0:T(1,128)} %param.22) | copy-start | bytes 24580
  17.7 29.2 %all-to-all-start = ((bf16[4,2,384]{2,1,0:T(2,128)(2,1)}), bf16[4,2,384]{2,1,0:T(2,128)(2,1)S(1)}, u32[]{:S(2)}, u32[]{:S(2)}) async-start(bf16[4,2,384]{2,1,0:T(2,128)(2,1)} %all_to_all.69), calls=%async_computation | async-start | bytes 12288 | tf_op jit(solution)/shard_map/all_to_all | solution.py:165
  66.8 10.1 %all-to-all-start.1 = ((f32[4,2,512]{2,1,0:T(2,128)}), f32[4,2,512]{2,1,0:T(2,128)S(1)}, u32[]{:S(2)}, u32[]{:S(2)}) async-start(f32[4,2,512]{2,1,0:T(2,128)} %pad_maximum_fusion), calls=%async_computation.1 | async-start | bytes 32768 | tf_op jit(solution)/shard_map/all_to_all | solution.py:194
  82.2 8.9 %all-to-all-start.2 = ((bf16[4,2,2048]{2,1,0:T(2,128)(2,1)}), bf16[4,2,2048]{2,1,0:T(2,128)(2,1)S(1)}, u32[]{:S(2)}, u32[]{:S(2)}) async-start(bf16[4,2,2048]{2,1,0:T(2,128)(2,1)} %broadcast_select_fusion.2), calls=%async_computation.2 | async-start | bytes 65536 | tf_op jit(solution)/shard_map/all_to_all | solution.py:217
  85.7 20.9 %copy-start.9 = (s32[2]{0:T(128)S(1)}, s32[2]{0:T(128)}, u32[]{:S(2)}) copy-start(s32[2]{0:T(128)} %get-tuple-element.11) | copy-start | bytes 28
  85.7 20.9 %copy-start.10 = (s32[2]{0:T(128)S(1)}, s32[2]{0:T(128)}, u32[]{:S(2)}) copy-start(s32[2]{0:T(128)} %get-tuple-element.12) | copy-start | bytes 28
  85.7 34.9 %copy-start.2 = (f32[1,2048]{1,0:T(1,128)S(1)}, f32[1,2048]{1,0:T(1,128)}, u32[]{:S(2)}) copy-start(f32[1,2048]{1,0:T(1,128)} %param.19) | copy-start | bytes 24580
  85.7 69.1 %copy-start.7 = (f32[2,64]{1,0:T(2,128)S(1)}, f32[2,64]{1,0:T(2,128)}, u32[]{:S(2)}) copy-start(f32[2,64]{1,0:T(2,128)} %get-tuple-element.94) | copy-start | bytes 1540
  85.7 69.1 %copy-start.8 = (f32[2,64]{1,0:T(2,128)S(1)}, f32[2,64]{1,0:T(2,128)}, u32[]{:S(2)}) copy-start(f32[2,64]{1,0:T(2,128)} %get-tuple-element.95) | copy-start | bytes 1540
  103.3 8.9 %all-to-all-start.3 = ((bf16[4,2,2048]{2,1,0:T(2,128)(2,1)}), bf16[4,2,2048]{2,1,0:T(2,128)(2,1)S(1)}, u32[]{:S(2)}, u32[]{:S(2)}) async-start(bf16[4,2,2048]{2,1,0:T(2,128)(2,1)} %copy.112), calls=%async_computation.3 | async-start | bytes 65536 | tf_op jit(solution)/shard_map/all_to_all | solution.py:228
  115.7 4.8 %collective-permute-start = (bf16[2,2048]{1,0:T(2,128)(2,1)S(1)}, bf16[2,2048]{1,0:T(2,128)(2,1)S(1)}, u32[]{:S(2)}, u32[]{:S(2)}) collective-permute-start(bf16[2,2048]{1,0:T(2,128)(2,1)S(1)} %fusion.112), channel_id=1, source_target_pairs={{0,1},{2,3},{4,5},{6,7},{8,9},{10,11},{12,13},{14,15},{16,17},{18,... | collective-permute-start | bytes 24584 | tf_op jit(solution)/shard_map/ppermute | solution.py:17
  134.7 20.1 %all-to-all-start.4 = ((bf16[4,2,384]{2,1,0:T(2,128)(2,1)}), bf16[4,2,384]{2,1,0:T(2,128)(2,1)S(1)}, u32[]{:S(2)}, u32[]{:S(2)}) async-start(bf16[4,2,384]{2,1,0:T(2,128)(2,1)} %all_to_all.76), calls=%async_computation.4 | async-start | bytes 12288 | tf_op jit(solution)/shard_map/all_to_all | solution.py:165
  173.4 10.1 %all-to-all-start.5 = ((f32[4,2,512]{2,1,0:T(2,128)}), f32[4,2,512]{2,1,0:T(2,128)S(1)}, u32[]{:S(2)}, u32[]{:S(2)}) async-start(f32[4,2,512]{2,1,0:T(2,128)} %pad_maximum_fusion.1), calls=%async_computation.5 | async-start | bytes 32768 | tf_op jit(solution)/shard_map/all_to_all | solution.py:194
  188.8 8.9 %all-to-all-start.6 = ((bf16[4,2,2048]{2,1,0:T(2,128)(2,1)}), bf16[4,2,2048]{2,1,0:T(2,128)(2,1)S(1)}, u32[]{:S(2)}, u32[]{:S(2)}) async-start(bf16[4,2,2048]{2,1,0:T(2,128)(2,1)} %broadcast_select_fusion.1), calls=%async_computation.6 | async-start | bytes 65536 | tf_op jit(solution)/shard_map/all_to_all | solution.py:217
  192.5 69.8 %copy-start.5 = (f32[2,64]{1,0:T(2,128)S(1)}, f32[2,64]{1,0:T(2,128)}, u32[]{:S(2)}) copy-start(f32[2,64]{1,0:T(2,128)} %get-tuple-element.85) | copy-start | bytes 1540
  192.5 69.8 %copy-start.6 = (f32[2,64]{1,0:T(2,128)S(1)}, f32[2,64]{1,0:T(2,128)}, u32[]{:S(2)}) copy-start(f32[2,64]{1,0:T(2,128)} %get-tuple-element.86) | copy-start | bytes 1540
  209.3 85.2 %copy-start.11 = (bf16[1,2048,4]{1,2,0:T(4,128)(2,1)S(1)}, bf16[1,2048,4]{1,2,0:T(4,128)(2,1)}, u32[]{:S(2)}) copy-start(bf16[1,2048,4]{1,2,0:T(4,128)(2,1)} %param.23) | copy-start | bytes 49156
  209.9 8.9 %all-to-all-start.7 = ((bf16[4,2,2048]{2,1,0:T(2,128)(2,1)}), bf16[4,2,2048]{2,1,0:T(2,128)(2,1)S(1)}, u32[]{:S(2)}, u32[]{:S(2)}) async-start(bf16[4,2,2048]{2,1,0:T(2,128)(2,1)} %copy.121), calls=%async_computation.7 | async-start | bytes 65536 | tf_op jit(solution)/shard_map/all_to_all | solution.py:228
  222.3 5.6 %collective-permute-start.1 = (bf16[2,2048]{1,0:T(2,128)(2,1)S(1)}, bf16[2,2048]{1,0:T(2,128)(2,1)S(1)}, u32[]{:S(2)}, u32[]{:S(2)}) collective-permute-start(bf16[2,2048]{1,0:T(2,128)(2,1)S(1)} %fusion.120), channel_id=1, source_target_pairs={{0,1},{2,3},{4,5},{6,7},{8,9},{10,11},{12,13},{14,15},{16,17},{18,... | collective-permute-start | bytes 24584 | tf_op jit(solution)/shard_map/ppermute | solution.py:17
  242.2 20.1 %all-to-all-start.8 = ((bf16[4,2,384]{2,1,0:T(2,128)(2,1)}), bf16[4,2,384]{2,1,0:T(2,128)(2,1)S(1)}, u32[]{:S(2)}, u32[]{:S(2)}) async-start(bf16[4,2,384]{2,1,0:T(2,128)(2,1)} %all_to_all.83), calls=%async_computation.8 | async-start | bytes 12288 | tf_op jit(solution)/shard_map/all_to_all | solution.py:165
  280.8 10.1 %all-to-all-start.9 = ((f32[4,2,512]{2,1,0:T(2,128)}), f32[4,2,512]{2,1,0:T(2,128)S(1)}, u32[]{:S(2)}, u32[]{:S(2)}) async-start(f32[4,2,512]{2,1,0:T(2,128)} %pad_maximum_fusion.2), calls=%async_computation.9 | async-start | bytes 32768 | tf_op jit(solution)/shard_map/all_to_all | solution.py:194
  295.5 8.9 %all-to-all-start.10 = ((bf16[4,2,2048]{2,1,0:T(2,128)(2,1)}), bf16[4,2,2048]{2,1,0:T(2,128)(2,1)S(1)}, u32[]{:S(2)}, u32[]{:S(2)}) async-start(bf16[4,2,2048]{2,1,0:T(2,128)(2,1)} %broadcast_select_fusion), calls=%async_computation.10 | async-start | bytes 65536 | tf_op jit(solution)/shard_map/all_to_all | solution.py:217
  316.6 8.9 %all-to-all-start.11 = ((bf16[4,2,2048]{2,1,0:T(2,128)(2,1)}), bf16[4,2,2048]{2,1,0:T(2,128)(2,1)S(1)}, u32[]{:S(2)}, u32[]{:S(2)}) async-start(bf16[4,2,2048]{2,1,0:T(2,128)(2,1)} %copy.130), calls=%async_computation.11 | async-start | bytes 65536 | tf_op jit(solution)/shard_map/all_to_all | solution.py:228
